TPU v7x, 32 devices: a whole 2x2x4 slice. The times are simulated.
32 devices in a mesh: dp: 4 (over x, y), tp: 8 (over z, core).
Axes of the slice: x: 2, y: 2, z: 4, core: 2. Of those that a mesh axis runs over, the one named last changes fastest.
Arguments:
- tok_ids: int32 [8, 2048], P('dp'), parts along dimension 0
- pad_mask: int32 [8, 2048], P('dp'), parts along dimension 0
- emb_table: bfloat16 [250880, 2048], P('tp')
- ln_emb_w: bfloat16 [2048], replicated
- ln_emb_b: bfloat16 [2048], replicated
- ln1_w: bfloat16 [2048], replicated
- ln1_b: bfloat16 [2048], replicated
- w_qkv: bfloat16 [2048, 16, 3, 128], P(None, 'tp')
- b_qkv: bfloat16 [16, 3, 128], P('tp')
- w_out: bfloat16 [2048, 2048], P('tp')
- b_out: bfloat16 [2048], replicated
- ln2_w: bfloat16 [2048], replicated
- ln2_b: bfloat16 [2048], replicated
- w_up: bfloat16 [2048, 8192], P(None, 'tp')
- b_up: bfloat16 [8192], P('tp')
- w_down: bfloat16 [8192, 2048], P('tp')
- b_down: bfloat16 [2048], replicated
Outputs:
- output: bfloat16 [8, 2048, 2048], P('dp', 'tp'), parts along dimension 0
There are 4 independent parts. A program takes and returns all parts, laid end to end along the dimension named above; an argument that names none is the same for every part.
All inputs are finite; a program needn't handle non-finite values.
Results may differ from a plain program's by a relative error of at most 0.014022.
Values are sent between devices in bfloat16 or wider.
A program may use at most 1 GiB of HBM per device.

v0:
```python
import functools
import math
import jax
import jax.numpy as jnp
from jax import lax
from jax.experimental import pallas as pl
from jax.experimental.pallas import tpu as pltpu
from jax.sharding import PartitionSpec as P

LN_EPS = 1e-5
LOG2E = 1.4426950408889634
MESH = pl.DeviceIdType.MESH


def alibi_slopes(n_heads):
    closest = 2 ** int(math.floor(math.log2(n_heads)))
    base_ratio = 2.0 ** (-(2.0 ** -(math.log2(closest) - 3)))
    extra_ratio = 2.0 ** (-(2.0 ** -(math.log2(2 * closest) - 3)))
    first_part = [base_ratio ** step_k for step_k in range(1, closest + 1)]
    second_part = [extra_ratio ** step_k for step_k in range(1, 2 * (n_heads - closest), 2)]
    return first_part + second_part


def bloom_gelu(values_in):
    return values_in * 0.5 * (1.0 + jnp.tanh(0.79788456 * values_in * (1.0 + 0.044715 * values_in * values_in)))


GROUP = 64
SUB = 32
SLOTS = 4


def lookup_kernel(tile_ref, sel_ref, table_ref, out_ref, buf, sems):
    step = pl.program_id(0)
    steps = pl.num_programs(0)

    def issue(grp):
        slot = lax.rem(grp, SLOTS)
        for i in range(GROUP):
            row = pl.multiple_of(tile_ref[grp * GROUP + i] * 8, 8)
            pltpu.make_async_copy(table_ref.at[pl.ds(row, 8), :], buf.at[slot, pl.ds(i * 8, 8), :], sems.at[slot]).start()

    @pl.when(step == 0)
    def _():
        for grp in range(SLOTS - 1):
            issue(grp)

    @pl.when(step + SLOTS - 1 < steps)
    def _():
        issue(step + SLOTS - 1)

    slot = lax.rem(step, SLOTS)
    pltpu.make_async_copy(table_ref.at[pl.ds(0, GROUP * 8), :], buf.at[slot], sems.at[slot]).wait()
    for j in range(GROUP // SUB):
        cols = lax.broadcasted_iota(jnp.int32, (SUB, SUB * 8), 1)
        onehot = (cols == sel_ref[pl.ds(j * SUB, SUB), :]).astype(jnp.float32).astype(jnp.bfloat16)
        rows = jnp.dot(onehot, buf[slot, pl.ds(j * SUB * 8, SUB * 8), :], preferred_element_type=jnp.float32)
        out_ref[pl.ds(j * SUB, SUB), :] = rows.astype(jnp.bfloat16)


def lookup(ids, table, tp_rank):
    n_tok = ids.shape[0]
    vocab_loc, d = table.shape
    loc = ids - tp_rank * vocab_loc
    held = (loc >= 0) & (loc < vocab_loc)
    spread = (jnp.arange(n_tok, dtype=jnp.int32) * 5) % (vocab_loc // 8)
    tile = jnp.where(held, loc // 8, spread)
    sel = jnp.where(held, (jnp.arange(n_tok, dtype=jnp.int32) % SUB) * 8 + loc % 8, -1)[:, None]
    return pl.pallas_call(
        lookup_kernel,
        out_shape=jax.ShapeDtypeStruct((n_tok, d), jnp.bfloat16),
        grid_spec=pltpu.PrefetchScalarGridSpec(
            num_scalar_prefetch=1,
            grid=(n_tok // GROUP,),
            in_specs=[pl.BlockSpec((GROUP, 1), lambda i, t: (i, 0)), pl.BlockSpec(memory_space=pl.ANY)],
            out_specs=pl.BlockSpec((GROUP, d), lambda i, t: (i, 0)),
            scratch_shapes=[pltpu.VMEM((SLOTS, GROUP * 8, d), jnp.bfloat16), pltpu.SemaphoreType.DMA((SLOTS,))],
        ),
        compiler_params=pltpu.CompilerParams(dimension_semantics=("arbitrary",)),
        cost_estimate=pl.CostEstimate(flops=n_tok * d * 40000, bytes_accessed=n_tok * d * 18, transcendentals=0),
        name="lookup",
    )(tile, sel, table)


CHUNK = 32
LAG = 3
LN_ROWS = 16


def norm_rows(x, gain, shift):
    n = x.shape[-1]
    mean_v = jnp.sum(x, axis=-1, keepdims=True) * (1.0 / n)
    centered = x - mean_v
    var_v = jnp.sum(centered * centered, axis=-1, keepdims=True) * (1.0 / n)
    return (centered * lax.rsqrt(var_v + LN_EPS) * gain + shift).astype(jnp.bfloat16)


def chain_kernel(n_tp, part_ref, ln_ref, a_ref, r0_ref, own, pre, rgt, lft, abuf, r0buf,
                 own_sem, pre_send, pre_recv, r_send, r_recv, l_send, l_recv, a_loc, a_send, a_recv, r0_loc, r0_send, r0_recv):
    seq = part_ref.shape[1]
    n_chunk = seq // CHUNK
    n_z = n_tp // 2
    me = lax.axis_index("tp")
    z = me // 2
    c = lax.rem(me, 2)
    peer = me + 1 - 2 * c
    pos_per = r0_ref.shape[1]
    per_dev = pos_per // CHUNK
    last = n_z - 1

    barrier = pltpu.get_barrier_semaphore()
    pl.semaphore_signal(barrier, inc=1, device_id={"tp": peer}, device_id_type=MESH)

    @pl.when(z > 0)
    def _():
        pl.semaphore_signal(barrier, inc=1, device_id={"tp": me - 2}, device_id_type=MESH)

    @pl.when(z < last)
    def _():
        pl.semaphore_signal(barrier, inc=1, device_id={"tp": me + 2}, device_id_type=MESH)

    @pl.when((z > 0) & (z < last))
    def _():
        pl.semaphore_wait(barrier, 3)

    @pl.when((z == 0) | (z == last))
    def _():
        pl.semaphore_wait(barrier, 2)

    def rows(k):
        return pl.ds(pl.multiple_of(k * CHUNK, CHUNK), CHUNK)

    def own_copy(k):
        return pltpu.make_async_copy(part_ref.at[c, rows(k), :], own.at[rows(k), :], own_sem.at[k])

    def pre_copy(k):
        return pltpu.make_async_remote_copy(part_ref.at[1 - c, rows(k), :], pre.at[rows(k), :], pre_send.at[k], pre_recv.at[k], device_id={"tp": peer}, device_id_type=MESH)

    def right_copy(src, k):
        return pltpu.make_async_remote_copy(src.at[rows(k), :], rgt.at[rows(k), :], r_send.at[k], r_recv.at[k], device_id={"tp": me + 2}, device_id_type=MESH)

    def left_copy(k):
        return pltpu.make_async_remote_copy(pre.at[rows(k), :], lft.at[rows(k), :], l_send.at[k], l_recv.at[k], device_id={"tp": me - 2}, device_id_type=MESH)

    def a_local(k):
        return pltpu.make_async_copy(abuf.at[rows(k), :], a_ref.at[c, rows(k), :], a_loc.at[k])

    def a_peer(k):
        return pltpu.make_async_remote_copy(abuf.at[rows(k), :], a_ref.at[c, rows(k), :], a_send.at[k], a_recv.at[k], device_id={"tp": peer}, device_id_type=MESH)

    def r0_local(i):
        return pltpu.make_async_copy(r0buf.at[c, rows(i), :], r0_ref.at[c, rows(i), :], r0_loc.at[i])

    def r0_peer(i):
        return pltpu.make_async_remote_copy(r0buf.at[1 - c, rows(i), :], r0_ref.at[c, rows(i), :], r0_send.at[i], r0_recv.at[i], device_id={"tp": peer}, device_id_type=MESH)

    def start(k, carry):
        own_copy(k).start()
        pre_copy(k).start()
        return carry

    lax.fori_loop(0, n_chunk, start, 0)

    def step_body(s, carry):
        @pl.when(s < n_chunk)
        def _():
            own_copy(s).wait()
            pre_copy(s).wait_recv()
            own[rows(s), :] = own[rows(s), :] + pre[rows(s), :]

        kr = s - LAG * z

        @pl.when((kr >= 0) & (kr < n_chunk))
        def _():
            @pl.when(z == 0)
            def _():
                right_copy(own, kr).start()

            @pl.when(z > 0)
            def _():
                right_copy(rgt, kr).wait_recv()
                rgt[rows(kr), :] = rgt[rows(kr), :] + own[rows(kr), :]

                @pl.when(z < last)
                def _():
                    right_copy(rgt, kr).start()

        kl = s - LAG * (last - z)

        @pl.when((kl >= 0) & (kl < n_chunk))
        def _():
            @pl.when(z < last)
            def _():
                left_copy(kl).wait_recv()

                @pl.when(z > 0)
                def _():
                    pre[rows(kl), :] = lft[rows(kl), :] + own[rows(kl), :]

            @pl.when(z == last)
            def _():
                pre[rows(kl), :] = own[rows(kl), :]

            @pl.when(z > 0)
            def _():
                left_copy(kl).start()

        kt = s - LAG * jnp.maximum(z, last - z)

        @pl.when((kt >= 0) & (kt < n_chunk))
        def _():
            base = kt * CHUNK
            first = kt - z * 2 * per_dev
            near = (first >= 0) & (first < 2 * per_dev)
            side = jnp.where(near, first // per_dev, 0)
            inner = jnp.where(near, lax.rem(first, per_dev), 0)

            def norm(i, carry):
                sl = pl.ds(pl.multiple_of(base + i * LN_ROWS, LN_ROWS), LN_ROWS)

                @pl.when(z == 0)
                def _():
                    abuf[sl, :] = own[sl, :] + lft[sl, :]

                @pl.when((z > 0) & (z < last))
                def _():
                    abuf[sl, :] = rgt[sl, :] + lft[sl, :]

                @pl.when(z == last)
                def _():
                    abuf[sl, :] = rgt[sl, :]

                r0 = norm_rows(abuf[sl, :].astype(jnp.float32), ln_ref[0:1, :], ln_ref[1:2, :])
                abuf[sl, :] = norm_rows(r0.astype(jnp.float32), ln_ref[2:3, :], ln_ref[3:4, :])

                @pl.when(near)
                def _():
                    r0buf[side, pl.ds(pl.multiple_of(inner * CHUNK + i * LN_ROWS, LN_ROWS), LN_ROWS), :] = r0

                return carry

            lax.fori_loop(0, CHUNK // LN_ROWS, norm, 0)
            a_local(kt).start()
            a_peer(kt).start()

            @pl.when(near & (side == c))
            def _():
                r0_local(inner).start()

            @pl.when(near & (side != c))
            def _():
                r0_peer(inner).start()

        return carry

    lax.fori_loop(0, n_chunk + LAG * last, step_body, 0)

    def drain(k, carry):
        pre_copy(k).wait_send()
        a_local(k).wait()
        a_peer(k).wait()

        @pl.when(z < last)
        def _():
            right_copy(rgt, k).wait_send()

        @pl.when(z > 0)
        def _():
            left_copy(k).wait_send()

        return carry

    lax.fori_loop(0, n_chunk, drain, 0)

    def drain_r0(i, carry):
        r0_local(i).wait()
        r0_peer(i).wait()
        return carry

    lax.fori_loop(0, per_dev, drain_r0, 0)


def chain(part, ln_pack, n_tp):
    n_seq, seq, d = part.shape
    n_chunk = seq // CHUNK
    per_dev = seq // n_tp // CHUNK
    dma = pltpu.SemaphoreType.DMA
    big = pltpu.VMEM((seq, d), jnp.bfloat16)
    return pl.pallas_call(
        functools.partial(chain_kernel, n_tp),
        out_shape=(jax.ShapeDtypeStruct((n_seq, seq, d), jnp.bfloat16), jax.ShapeDtypeStruct((n_seq, seq // n_tp, d), jnp.bfloat16)),
        in_specs=[pl.BlockSpec(memory_space=pl.ANY), pl.BlockSpec(memory_space=pltpu.VMEM)],
        out_specs=(pl.BlockSpec(memory_space=pl.ANY), pl.BlockSpec(memory_space=pl.ANY)),
        scratch_shapes=[big, big, big, big, big, pltpu.VMEM((2, seq // n_tp, d), jnp.bfloat16)]
        + [dma((n_chunk,))] * 10 + [dma((per_dev,))] * 3,
        compiler_params=pltpu.CompilerParams(collective_id=0, has_side_effects=True, vmem_limit_bytes=58 * 1024 * 1024),
        cost_estimate=pl.CostEstimate(flops=10 ** 6, bytes_accessed=8 * part.size, transcendentals=0),
        name="chain",
    )(part, ln_pack)


def attend_kernel(n_tp, head_dim, qkv_ref, pad_ref, slope_ref, bup_ref, ctx_ref, ball_ref, cbuf, send_sem, recv_sem, loc_sem, b_send, b_recv, b_loc):
    n_seq, heads = qkv_ref.shape[1], qkv_ref.shape[2]
    seq = qkv_ref.shape[3]
    blk = seq // n_tp
    feat = heads * head_dim
    me = lax.axis_index("tp")

    barrier = pltpu.get_barrier_semaphore()
    for r in range(1, n_tp):
        pl.semaphore_signal(barrier, inc=1, device_id={"tp": lax.rem(me + r, n_tp)}, device_id_type=MESH)
    pl.semaphore_wait(barrier, n_tp - 1)

    def cols(t):
        return pl.ds(pl.multiple_of(t * feat, feat), feat)

    def bias_copy(r):
        return pltpu.make_async_remote_copy(bup_ref, ball_ref.at[me], b_send.at[r], b_recv.at[r], device_id={"tp": lax.rem(me + r, n_tp)}, device_id_type=MESH)

    for r in range(1, n_tp):
        bias_copy(r).start()
    own_bias = pltpu.make_async_copy(bup_ref, ball_ref.at[me], b_loc.at[0])
    own_bias.start()

    def ctx_copy(b, r):
        return pltpu.make_async_remote_copy(cbuf.at[b, r], ctx_ref.at[b, :, cols(me)], send_sem.at[b, r], recv_sem.at[b, r], device_id={"tp": lax.rem(me + r, n_tp)}, device_id_type=MESH)

    def ctx_local(b):
        return pltpu.make_async_copy(cbuf.at[b, 0], ctx_ref.at[b, :, cols(me)], loc_sem.at[b])

    def one(i, carry):
        b = lax.rem(i, n_seq)
        r = n_tp - 1 - i // n_seq
        dest = lax.rem(me + r, n_tp)
        for j in range(n_tp):
            @pl.when(dest == j)
            def _(j=j):
                span = (j + 1) * blk
                lo = j * blk
                key_pos = lax.broadcasted_iota(jnp.int32, (1, span), 1)
                key_ok = pad_ref[b, :, 0:span] == 1
                row_in = lax.broadcasted_iota(jnp.int32, (blk, blk), 0)
                col_in = lax.broadcasted_iota(jnp.int32, (blk, blk), 1)
                diag_ok = ((col_in < row_in) & (pad_ref[b, :, lo:span] == 1)) | (col_in == row_in)
                for h in range(heads):
                    slope = slope_ref[0, h] * LOG2E
                    rel = slope * (key_pos - lo).astype(jnp.float32)
                    far = jnp.where(key_ok, rel, -1e30)
                    q = qkv_ref[0, b, h, lo:span, :]
                    scale = head_dim ** -0.5 * LOG2E
                    diag = lax.dot_general(q, qkv_ref[1, b, h, lo:span, :], (((1,), (1,)), ((), ())), preferred_element_type=jnp.float32)
                    diag = jnp.where(diag_ok, diag * scale + rel[:, lo:span], -1e30)
                    top = jnp.max(diag, axis=-1, keepdims=True)
                    if j:
                        past = lax.dot_general(q, qkv_ref[1, b, h, 0:lo, :], (((1,), (1,)), ((), ())), preferred_element_type=jnp.float32)
                        past = past * scale + far[:, 0:lo]
                        top = jnp.maximum(top, jnp.max(past, axis=-1, keepdims=True))
                        past = jnp.exp2(past - top)
                    diag = jnp.exp2(diag - top)
                    total = jnp.sum(diag, axis=-1, keepdims=True)
                    if j:
                        total = total + jnp.sum(past, axis=-1, keepdims=True)
                    inv = 1.0 / total
                    out = jnp.dot((diag * inv).astype(jnp.bfloat16), qkv_ref[2, b, h, lo:span, :], preferred_element_type=jnp.float32)
                    if j:
                        out = out + jnp.dot((past * inv).astype(jnp.bfloat16), qkv_ref[2, b, h, 0:lo, :], preferred_element_type=jnp.float32)
                    cbuf[b, r, :, h * head_dim:(h + 1) * head_dim] = out.astype(jnp.bfloat16)

        @pl.when(r > 0)
        def _():
            ctx_copy(b, r).start()

        @pl.when(r == 0)
        def _():
            ctx_local(b).start()

        return carry

    lax.fori_loop(0, n_seq * n_tp, one, 0)

    for b in range(n_seq):
        ctx_local(b).wait()
        for r in range(1, n_tp):
            ctx_copy(b, r).wait()
    own_bias.wait()
    for r in range(1, n_tp):
        bias_copy(r).wait()


def attend(qkv, pad_mask, slopes, b_up, n_tp):
    _, n_seq, heads, seq, head_dim = qkv.shape
    blk = seq // n_tp
    feat = heads * head_dim
    dma = pltpu.SemaphoreType.DMA
    vmem = pl.BlockSpec(memory_space=pltpu.VMEM)
    return pl.pallas_call(
        functools.partial(attend_kernel, n_tp, head_dim),
        out_shape=(jax.ShapeDtypeStruct((n_seq, blk, n_tp * feat), jnp.bfloat16), jax.ShapeDtypeStruct((n_tp,) + b_up.shape, jnp.bfloat16)),
        in_specs=[vmem, vmem, pl.BlockSpec(memory_space=pltpu.SMEM), vmem],
        out_specs=(pl.BlockSpec(memory_space=pl.ANY), pl.BlockSpec(memory_space=pl.ANY)),
        scratch_shapes=[pltpu.VMEM((n_seq, n_tp, blk, feat), jnp.bfloat16), dma((n_seq, n_tp)), dma((n_seq, n_tp)), dma((n_seq,)), dma((n_tp,)), dma((n_tp,)), dma((1,))],
        compiler_params=pltpu.CompilerParams(collective_id=1, has_side_effects=True, vmem_limit_bytes=56000 * 1024),
        cost_estimate=pl.CostEstimate(flops=30 * 10 ** 9, bytes_accessed=2 * qkv.size, transcendentals=seq * seq * 2),
        name="attend",
    )(qkv, pad_mask[:, None, :], slopes[None, :], b_up)


SUBROWS = 128


def mlp_kernel(n_dp, ctx_ref, r0_ref, wo_ref, wup_ref, wdn_ref, fup_ref, fdn_ref, bias_ref, vec_ref, out_ref,
               ctx, r0, r1, wo_w, xbuf, ptl, up_w, dn_w, act, from_peer, pre, from_far, obuf,
               w_sem, x_sem, px_send, px_recv, fx_send, fx_recv, fw_send, fw_recv, lp_send, lp_recv, pr_send, pr_recv, rf_send, rf_recv, o_sem):
    me = lax.axis_index("tp")
    peer = me + 1 - 2 * lax.rem(me, 2)
    far = me + 2 - 4 * lax.rem(me // 2, 2)
    mid = 2 * SUBROWS
    n_loc = ctx.shape[0] // mid
    n_sub = ctx.shape[0] // SUBROWS
    steps = 2 * n_loc + n_sub
    first_far = 2 * n_loc
    wide = up_w.shape[2]
    n_up = wup_ref.shape[1] // wide
    n_blk = up_w.shape[0]
    d_loc = wdn_ref.shape[0]
    slim = fup_ref.shape[2]

    barrier = pltpu.get_barrier_semaphore()
    pl.semaphore_signal(barrier, inc=1, device_id={"tp": peer}, device_id_type=MESH)
    pl.semaphore_signal(barrier, inc=1, device_id={"tp": far}, device_id_type=MESH)

    first = [pltpu.make_async_copy(src, dst, x_sem.at[i]) for i, (src, dst) in enumerate([(ctx_ref, ctx), (r0_ref, r0), (wo_ref, wo_w)])]
    for load in first:
        load.start()
    loads = []
    for i in range(n_up):
        loads.append(pltpu.make_async_copy(wup_ref.at[:, pl.ds(i * wide, wide)], up_w.at[i], w_sem.at[len(loads)]))
    for i in range(n_dp):
        loads.append(pltpu.make_async_copy(fup_ref.at[i], up_w.at[n_up + i * slim // wide, :, pl.ds(i * slim % wide, slim)], w_sem.at[len(loads)]))
    loads.append(pltpu.make_async_copy(wdn_ref, dn_w.at[pl.ds(0, d_loc), :], w_sem.at[len(loads)]))
    loads.append(pltpu.make_async_copy(fdn_ref, dn_w.at[pl.ds(d_loc, d_loc), :], w_sem.at[len(loads)]))
    pl.semaphore_wait(barrier, 2)

    def remote(src, dst, send, recv, to):
        return pltpu.make_async_remote_copy(src, dst, send, recv, device_id={"tp": to}, device_id_type=MESH)

    def sub(i):
        return pl.ds(pl.multiple_of(i * SUBROWS, SUBROWS), SUBROWS)

    def x_far(i):
        return remote(xbuf.at[i // 2, sub(lax.rem(i, 2)), :], xbuf.at[first_far + i, pl.ds(0, SUBROWS), :], fx_send.at[i], fx_recv.at[i], far)

    def x_peer(i):
        return remote(xbuf.at[i], xbuf.at[n_loc + i], px_send.at[i], px_recv.at[i], peer)

    def x_pass(i):
        return remote(xbuf.at[first_far + i, pl.ds(0, SUBROWS), :], xbuf.at[first_far + i, pl.ds(SUBROWS, SUBROWS), :], fw_send.at[i], fw_recv.at[i], peer)

    def back_peer(i):
        return remote(ptl.at[n_loc + i], from_peer.at[i], lp_send.at[i], lp_recv.at[i], peer)

    def back_pre(i):
        return remote(ptl.at[first_far + i, pl.ds(SUBROWS, SUBROWS), :], pre.at[i], pr_send.at[i], pr_recv.at[i], peer)

    def back_far(i):
        return remote(ptl.at[first_far + i, pl.ds(0, SUBROWS), :], from_far.at[i], rf_send.at[i], rf_recv.at[i], far)

    for load in first:
        load.wait()
    for load in loads:
        load.start()

    def project(i, carry):
        for g in range(n_dp):
            sl = pl.ds(g * wo_w.shape[2], wo_w.shape[2])
            attn = jnp.dot(ctx[sub(i), :], wo_w[g], preferred_element_type=jnp.float32)
            r1[sub(i), sl] = (r0[sub(i), sl].astype(jnp.float32) + (attn + vec_ref[0:1, sl])).astype(jnp.bfloat16)
        for r in range(0, SUBROWS, 16):
            rows = r1[pl.ds(pl.multiple_of(i * SUBROWS + r, 16), 16), :].astype(jnp.float32)
            xbuf[i // 2, pl.ds(pl.multiple_of(lax.rem(i, 2) * SUBROWS + r, 16), 16), :] = norm_rows(rows, vec_ref[1:2, :], vec_ref[2:3, :])
        x_far(i).start()

        @pl.when(lax.rem(i, 2) == 1)
        def _():
            x_peer(i // 2).start()

        return carry

    lax.fori_loop(0, n_sub, project, 0)
    for load in loads:
        load.wait()

    def body(s, carry):
        @pl.when((s >= 2) & (s < 2 + n_sub))
        def _():
            x_far(s - 2).wait_recv()
            x_pass(s - 2).start()

        @pl.when((s >= n_loc) & (s < first_far))
        def _():
            x_peer(s - n_loc).wait_recv()

        @pl.when((s >= first_far) & (s < steps))
        def _():
            x_pass(s - first_far).wait_recv()

        @pl.when(s < steps)
        def _():
            def up(n, carry):
                hid = jnp.dot(xbuf[s], up_w[n], preferred_element_type=jnp.float32) + bias_ref[n]
                act[:, pl.ds(pl.multiple_of(n * wide, wide), wide)] = bloom_gelu(hid).astype(jnp.bfloat16)
                return carry

            lax.fori_loop(0, n_blk, up, 0)

            def down(n, carry):
                sl = pl.ds(pl.multiple_of(n * wide, wide), wide)
                ptl[s, :, sl] = jnp.dot(act[...], dn_w[:, sl], preferred_element_type=jnp.float32).astype(jnp.bfloat16)
                return carry

            lax.fori_loop(0, dn_w.shape[1] // wide, down, 0)

        @pl.when((s >= n_loc) & (s < first_far))
        def _():
            back_peer(s - n_loc).start()

        @pl.when((s >= first_far) & (s < steps))
        def _():
            back_pre(s - first_far).start()

        @pl.when(s > first_far)
        def _():
            i = s - first_far - 1
            back_pre(i).wait_recv()
            for r in range(0, SUBROWS, 32):
                sl = pl.ds(r, 32)
                ptl[first_far + i, sl, :] = (ptl[first_far + i, sl, :].astype(jnp.float32) + pre[i, sl, :].astype(jnp.float32)).astype(jnp.bfloat16)
            back_far(i).start()

        return carry

    lax.fori_loop(0, steps + 1, body, 0)

    for i in range(n_loc):
        back_peer(i).wait_recv()

    def out_copy(i):
        return pltpu.make_async_copy(obuf.at[sub(i), :], out_ref.at[sub(i), :], o_sem.at[i])

    def finish(i, carry):
        back_far(i).wait_recv()
        for r in range(0, SUBROWS, 16):
            own = pl.ds(pl.multiple_of(lax.rem(i, 2) * SUBROWS + r, 16), 16)
            row = pl.ds(pl.multiple_of(i * SUBROWS + r, 16), 16)
            total = ptl[i // 2, own, :].astype(jnp.float32) + from_peer[i // 2, own, :].astype(jnp.float32) + from_far[i, pl.ds(r, 16), :].astype(jnp.float32)
            obuf[row, :] = (r1[row, :].astype(jnp.float32) + (total + vec_ref[3:4, :])).astype(jnp.bfloat16)
        out_copy(i).start()
        return carry

    lax.fori_loop(0, n_sub, finish, 0)
    for i in range(n_loc):
        x_peer(i).wait_send()
        back_peer(i).wait_send()
    for i in range(n_sub):
        x_far(i).wait_send()
        x_pass(i).wait_send()
        back_pre(i).wait_send()
        back_far(i).wait_send()
        out_copy(i).wait()


def mlp(context, r0, wo, w_up, w_down, far_up, far_down, bias, vecs):
    rows, d = context.shape
    ff = w_up.shape[1]
    wide = 512
    mid = 2 * SUBROWS
    n_loc, n_sub = rows // mid, rows // SUBROWS
    steps = 2 * n_loc + n_sub
    n_dp = far_up.shape[0]
    bf = jnp.bfloat16
    dma = pltpu.SemaphoreType.DMA
    hbm = pl.BlockSpec(memory_space=pl.ANY)
    vmem = pl.BlockSpec(memory_space=pltpu.VMEM)
    return pl.pallas_call(
        functools.partial(mlp_kernel, n_dp),
        out_shape=jax.ShapeDtypeStruct((rows, d), bf),
        in_specs=[hbm] * 7 + [vmem] * 2,
        out_specs=hbm,
        scratch_shapes=[
            pltpu.VMEM((rows, d), bf), pltpu.VMEM((rows, d), bf), pltpu.VMEM((rows, d), bf), pltpu.VMEM(wo.shape, bf), pltpu.VMEM((steps, mid, d), bf), pltpu.VMEM((steps, mid, d), bf), pltpu.VMEM((2 * ff // wide, d, wide), bf), pltpu.VMEM((2 * ff, d), bf),
            pltpu.VMEM((mid, 2 * ff), bf), pltpu.VMEM((n_loc, mid, d), bf), pltpu.VMEM((n_sub, SUBROWS, d), bf), pltpu.VMEM((n_sub, SUBROWS, d), bf), pltpu.VMEM((rows, d), bf),
            dma((32,)), dma((3,)), dma((n_loc,)), dma((n_loc,)), dma((n_sub,)), dma((n_sub,)), dma((n_sub,)), dma((n_sub,)),
            dma((n_loc,)), dma((n_loc,)), dma((n_sub,)), dma((n_sub,)), dma((n_sub,)), dma((n_sub,)), dma((n_sub,)),
        ],
        compiler_params=pltpu.CompilerParams(collective_id=2, has_side_effects=True, vmem_limit_bytes=61900 * 1024),
        cost_estimate=pl.CostEstimate(flops=10 ** 12, bytes_accessed=40 * 10 ** 6, transcendentals=0),
        name="mlp",
    )(context, r0, wo, w_up, w_down, far_up, far_down, bias.reshape(2 * ff // wide, 1, wide), vecs)


def solution(mesh):
    n_tp = mesh.shape['tp']
    n_dp = mesh.shape['dp']

    def local_step(tok_ids, pad_mask, emb_shard, ln_emb_w, ln_emb_b, ln1_w, ln1_b, w_qkv, b_qkv, w_out, b_out, ln2_w, ln2_b, w_up, b_up, w_down, b_down):
        f32 = jnp.float32
        tp_rank = lax.axis_index('tp')
        dp_rank = lax.axis_index('dp')
        n_seq, seq = tok_ids.shape
        d = emb_shard.shape[1]
        heads_loc = w_qkv.shape[1]

        def part(w, axis):
            size = w.shape[axis] // n_dp
            return lax.dynamic_slice_in_dim(w, dp_rank * size, size, axis)

        half = n_tp // 2
        swap = [(t, (t + half) % n_tp) for t in range(n_tp)]
        out_part = lax.all_gather(part(w_out, 1), 'tp', axis=0, tiled=True)
        up_part = lax.ppermute(part(w_up, 1), 'tp', swap)
        down_part = lax.ppermute(part(w_down, 0), 'tp', swap)

        part_emb = lookup(tok_ids.reshape(-1), emb_shard, tp_rank)
        part_emb = part_emb.reshape(n_seq, seq, d)
        part_emb, up_part, out_part = lax.optimization_barrier((part_emb, up_part, out_part))
        wo = lax.all_gather(out_part, 'dp', axis=0, tiled=False)
        wu = lax.all_gather(up_part, 'dp', axis=0, tiled=False)
        ln_pack = jnp.stack([ln_emb_w, ln_emb_b, ln1_w, ln1_b]).astype(f32)
        normed_all, resid_in = chain(part_emb, ln_pack, n_tp)
        normed_all, wu, wo, down_part = lax.optimization_barrier((normed_all, wu, wo, down_part))
        wd = lax.all_gather(down_part, 'dp', axis=0, tiled=True)
        qkv = (jnp.einsum('bsd,dhce->cbhse', normed_all, w_qkv, preferred_element_type=f32) + b_qkv.astype(f32).transpose(1, 0, 2)[:, None, :, None, :]).astype(jnp.bfloat16)
        all_slopes = jnp.array(alibi_slopes(heads_loc * n_tp), f32)
        head_slopes = lax.dynamic_slice_in_dim(all_slopes, tp_rank * heads_loc, heads_loc)
        context, b_all = attend(qkv, pad_mask, head_slopes, b_up.reshape(8, -1), n_tp)
        context, wd = lax.optimization_barrier((context, wd))
        far_bias = lax.dynamic_index_in_dim(b_all, (tp_rank + half) % n_tp, 0, keepdims=False).reshape(-1)
        bias = jnp.concatenate([b_up, far_bias]).astype(f32)
        rows = n_seq * seq // n_tp
        vecs = jnp.stack([b_out, ln2_w, ln2_b, b_down]).astype(f32)
        out = mlp(context.reshape(rows, d), resid_in.reshape(rows, d), wo, w_up, w_down, wu, wd, bias, vecs)
        return out.reshape(n_seq, seq // n_tp, d)

    replicated = P(None)
    in_specs = (P('dp', None), P('dp', None), P('tp', None), replicated, replicated, replicated, replicated, P(None, 'tp', None, None), P('tp', None, None), P('tp', None), replicated, replicated, replicated, P(None, 'tp'), P('tp'), P('tp', None), replicated)
    return jax.shard_map(local_step, mesh=mesh, in_specs=in_specs, out_specs=P('dp', 'tp', None), check_vma=False)
```

profile of v0, /device:TPU:0, one launch (start us, length us, event | category | flops | bytes accessed | tf_op | source)
XLA Modules:
  0.0 510.8 jit_solution(6499605844385382090)
XLA Ops:
  6.5 2.4 constant_dynamic-slice_fusion.3
  9.0 4.1 collective-permute-start
  13.0 1.7 constant_dynamic-slice_fusion.2
  14.7 0.0 all-gather.7.cloned.1.call-update
  14.7 0.0 all-gather.11.cloned.1.call-start
  14.9 2.0 copy.37
  16.8 4.2 fusion.8.sel_ref
  21.0 0.6 fusion.16.tile_ref
  21.6 55.9 %lookup.1 = bf16[4096,2048]{1,0:T(8,128)(2,1)} custom-call(s32[4096]{0:T(1024)} %fusion.16.tile_ref, s32[4096,1]{1,0:T(8,128)} %fusion.8.sel_ref, bf16[31360,2048]{1,0:T(8,128)(2,1)} %table_ref.1), custom_call_target="tpu_custom_call" | custom-call | flops 335544320000 | bytes 150994944 | tf_op jit(solution)/shard_map/lookup/pallas_call | solution.py:69
  77.6 0.0 all-gather.7.cloned.1.call-done
  77.6 0.0 all-gather.11.cloned.1.call-update
  77.6 0.0 copy-start.4
  77.6 0.0 copy-start.5
  77.8 0.0 copy-start.14
  77.8 0.0 all-gather.13.cloned.1.call-start
  77.8 0.7 all-gather.13.cloned.1.call-update
  78.5 0.0 all-gather.9.cloned.1.call-start
  78.6 2.3 constant_dynamic-slice_fusion.1
  81.0 0.6 broadcast_in_dim.13.pad_ref
  81.7 0.6 dynamic-slice_bitcast_fusion.slope_ref
  82.3 0.6 maximum_convert_fusion.ln_ref
  83.0 0.6 maximum_convert_fusion.1.vec_ref
  83.6 237.1 %chain.1 = (bf16[2,2048,2048]{2,1,0:T(8,128)(2,1)}, bf16[2,256,2048]{2,1,0:T(8,128)(2,1)}) custom-call(bf16[2,2048,2048]{2,1,0:T(8,128)(2,1)} %bitcast.47, f32[4,2048]{1,0:T(4,128)} %maximum_convert_fusion.ln_ref), custom_call_target="tpu_custom_call" | custom-call | flops 1000000 | bytes 67108864 | tf_op jit(solution)/shard_map/chain/pallas_call | solution.py:289
  320.8 0.0 all-gather.11.cloned.1.call-done
  320.8 0.0 all-gather.13.cloned.1.call-done
  320.8 0.0 all-gather.9.cloned.1.call-update
  320.9 18.7 %fusion.2.qkv_ref = bf16[3,2,2,2048,128]{4,3,2,1,0:T(8,128)(2,1)} fusion(f32[3,2,128]{2,1,0:T(2,128)S(1)} %convert_bitcast_fusion, bf16[2,2048,2048]{2,1,0:T(8,128)(2,1)} %get-tuple-element.22, bf16[2048,2,3,128,1]{3,1,2,0,4:T(2,128)(2,1)S(1)} %bitcast.46), kind=kOutput, calls=%fused_computation.3 | convolution fusion | flops 12891193344 | bytes 26217472 | tf_op jit(solution)/shard_map/bsd,dhce->cbhse/dot_general | solution.py:632
  339.5 54.3 %attend.1 = (bf16[2,256,2048]{2,1,0:T(8,128)(2,1)}, bf16[8,8,128]{2,1,0:T(8,128)(2,1)}) custom-call(bf16[3,2,2,2048,128]{4,3,2,1,0:T(8,128)(2,1)} %fusion.2.qkv_ref, s32[2,1,2048]{2,1,0:T(1,128)} %broadcast_in_dim.13.pad_ref, f32[1,2]{1,0:T(1,128)} %dynamic-slice_bitcast_fusion.slope_ref, bf16[8,128]{1,0:T(8,128)(2,1)} %bitcast.51), custom_call_target="tpu_custom_call" | custom-call | flops 30000001024 | bytes 6291456 | tf_op jit(solution)/shard_map/attend/pallas_call | solution.py:396
  393.9 0.7 constant_dynamic-slice_fusion
  394.5 0.6 maximum_convert_fusion.2.bias_ref
  395.2 105.8 %mlp.1 = bf16[512,2048]{1,0:T(8,128)(2,1)} custom-call(bf16[512,2048]{1,0:T(8,128)(2,1)} %bitcast.55, bf16[512,2048]{1,0:T(8,128)(2,1)} %bitcast.54, bf16[4,2048,512]{2,1,0:T(8,128)(2,1)} %bitcast.52, bf16[2048,1024]{1,0:T(8,128)(2,1)} %wup_ref.1, bf16[1024,2048]{1,0:T(8,128)(2,1)} %wdn_ref.1, bf16[4,2048,256]{2,1,0:T(8,128)(2,1)} %bitcast.53, ...), custom_call_target="tpu_custom_call" | custom-call | flops 999999995904 | bytes 40000000 | tf_op jit(solution)/shard_map/mlp/pallas_call | solution.py:584
  501.0 3.3 copy.41
  (46 shorter events, 0.2 us)
Async XLA Ops:
  6.5 314.3 %copy-start = (bf16[2048,2,3,128]{3,1,2,0:T(2,128)(2,1)S(1)}, bf16[2048,2,3,128]{3,1,2,0:T(2,128)(2,1)}, u32[]{:S(2)}) copy-start(bf16[2048,2,3,128]{3,1,2,0:T(2,128)(2,1)} %param.25) | copy-start | bytes 9437188
  6.5 8.3 %copy-start.2 = (s32[2,2048]{1,0:T(2,128)S(1)}, s32[2,2048]{1,0:T(2,128)}, u32[]{:S(2)}) copy-start(s32[2,2048]{1,0:T(2,128)} %param.18) | copy-start | bytes 49156
  6.5 71.1 %all-gather.7.cloned.1.call-start = ((), (), s32[]{:S(2)}) async-start(), calls=%async_computation | async-start | bytes 2359296 | tf_op jit(solution)/shard_map/all_gather | solution.py:619
  9.0 68.6 %collective-permute-start = (bf16[2048,256]{1,0:T(8,128)(2,1)}, bf16[2048,256]{1,0:T(8,128)(2,1)}, u32[]{:S(2)}, u32[]{:S(2)}) collective-permute-start(bf16[2048,256]{1,0:T(8,128)(2,1)} %constant_dynamic-slice_fusion.3), channel_id=1, source_target_pairs={{0,4},{1,5},{2,6},{3,7},{4,0},{5,1},{6,2},{7,3},{8,12},{9,13},{10,... | collective-permute-start | bytes 3145736 | tf_op jit(solution)/shard_map/ppermute | solution.py:620
  14.7 306.1 %all-gather.11.cloned.1.call-start = ((), (), s32[]{:S(2)}) async-start(), calls=%async_computation.2 | async-start | bytes 5242880 | tf_op jit(solution)/shard_map/all_gather | solution.py:627
  77.6 3.2 copy-start.4
  77.6 3.2 copy-start.5
  77.7 3.3 copy-start.6
  77.7 3.3 copy-start.7
  77.7 3.3 copy-start.3
  77.7 3.9 copy-start.12
  77.7 3.9 copy-start.8
  77.7 3.9 copy-start.9
  77.7 3.9 copy-start.10
  77.7 3.9 copy-start.11
  77.8 3.9 copy-start.14
  77.8 4.6 copy-start.13
  77.8 243.0 %all-gather.13.cloned.1.call-start = ((), (), s32[]{:S(2)}) async-start(), calls=%async_computation.3 | async-start | bytes 10485760 | tf_op jit(solution)/shard_map/all_gather | solution.py:626
  78.5 316.6 %all-gather.9.cloned.1.call-start = ((), (), s32[]{:S(2)}) async-start(), calls=%async_computation.1 | async-start | bytes 5242880 | tf_op jit(solution)/shard_map/all_gather | solution.py:631
  80.9 239.9 %collective-permute-start.1 = (bf16[256,2048]{1,0:T(8,128)(2,1)}, bf16[256,2048]{1,0:T(8,128)(2,1)}, u32[]{:S(2)}, u32[]{:S(2)}) collective-permute-start(bf16[256,2048]{1,0:T(8,128)(2,1)} %constant_dynamic-slice_fusion.1), channel_id=1, source_target_pairs={{0,4},{1,5},{2,6},{3,7},{4,0},{5,1},{6,2},{7,3},{8,12},{9,13},{10,... | collective-permute-start | bytes 3145736 | tf_op jit(solution)/shard_map/ppermute | solution.py:621
  501.0 3.3 copy-start.1
Sparse Core Ops, SparseCore 0:
  14.9 49.4 all-gather.6
  77.8 52.0 all-gather.10
  131.7 87.7 all-gather.12
  321.0 51.9 all-gather.8
where the time goes:
time: 515 us; the launch traced here: 511 us
  Pallas kernels  453 us (88%)
  matrix products  18.7 us (4%)
  local copies, waits for them, and re-layouts  13.8 us (3%)
  between operations  13.5 us (3%)
  other arithmetic  6.74 us (1%)
    pallas_call x1, Pallas kernels, chain(): pl.pallas_call(functools.partial(chain_kernel, n_tp), out_shape=(jax.Shap...  237 us
    pallas_call x1, Pallas kernels, mlp(): pl.pallas_call(functools.partial(mlp_kernel, n_dp), out_shape=jax.ShapeDt...  106 us
    pallas_call x1, Pallas kernels, lookup(): pl.pallas_call(lookup_kernel, out_shape=jax.ShapeDtypeStruct((n_tok, d),...  55.9 us
    pallas_call x1, Pallas kernels, attend(): pl.pallas_call(functools.partial(attend_kernel, n_tp, head_dim), out_shap...  54.3 us
    dot_general x1, matrix products, local_step(): jnp.einsum('bsd,dhce->cbhse', normed_all, w_qkv, preferred_element_type=f32)  18.7 us
  transfers between devices with their start and end apart: 6, of which 0 were waited for; matrix products, arithmetic and copies ran while one was open for 7% of the time, Pallas kernels for 68%

commit v1 on v0

--- a/solution.py
+++ b/solution.py
@@ -83,7 +83,7 @@
 
 
 CHUNK = 32
-LAG = 3
+LAG = 2
 LN_ROWS = 16
 
 
@@ -330,7 +330,8 @@
 
     def one(i, carry):
         b = lax.rem(i, n_seq)
-        r = n_tp - 1 - i // n_seq
+        turn = i // n_seq
+        r = n_tp // 2 + (turn + 1) // 2 * (1 - 2 * lax.rem(turn, 2))
         dest = lax.rem(me + r, n_tp)
         for j in range(n_tp):
             @pl.when(dest == j)

time: 515 us -> 514 us (level)
    pallas_call x1, Pallas kernels: 54.3 us -> 45.8 us  [attend(): pl.pallas_call(functools.partial(attend_kernel, n_tp, head_dim), out_shap...]
    pallas_call x1, Pallas kernels: 106 us -> 113 us  [mlp(): pl.pallas_call(functools.partial(mlp_kernel, n_dp), out_shape=jax.ShapeDt...]
  transfers between devices with their start and end apart: 6 -> 6, of which waited for: 0 -> 0; matrix products, arithmetic and copies ran while one was open for 7% -> 7% of each run, Pallas kernels for 68% -> 66%
where the time goes in v1:
time: 514 us; the launch traced here: 510 us
  Pallas kernels  452 us (88%)
  matrix products  18.7 us (4%)
  local copies, waits for them, and re-layouts  13.8 us (3%)
  between operations  13.5 us (3%)
  other arithmetic  6.74 us (1%)
    pallas_call x1, Pallas kernels, chain(): pl.pallas_call(functools.partial(chain_kernel, n_tp), out_shape=(jax.Shap...  238 us
    pallas_call x1, Pallas kernels, mlp(): pl.pallas_call(functools.partial(mlp_kernel, n_dp), out_shape=jax.ShapeDt...  113 us
    pallas_call x1, Pallas kernels, lookup(): pl.pallas_call(lookup_kernel, out_shape=jax.ShapeDtypeStruct((n_tok, d),...  55.9 us
    pallas_call x1, Pallas kernels, attend(): pl.pallas_call(functools.partial(attend_kernel, n_tp, head_dim), out_shap...  45.8 us
    dot_general x1, matrix products, local_step(): jnp.einsum('bsd,dhce->cbhse', normed_all, w_qkv, preferred_element_type=f32)  18.7 us
  transfers between devices with their start and end apart: 6, of which 0 were waited for; matrix products, arithmetic and copies ran while one was open for 7% of the time, Pallas kernels for 66%

profile of v1, /device:TPU:0, one launch (start us, length us, event | category | flops | bytes accessed | tf_op | source)
XLA Modules:
  0.0 510.1 jit_solution(9480841294328846449)
XLA Ops:
  6.5 2.4 constant_dynamic-slice_fusion.3
  9.0 4.1 collective-permute-start
  13.0 1.7 constant_dynamic-slice_fusion.2
  14.7 0.0 all-gather.7.cloned.1.call-update
  14.7 0.0 all-gather.11.cloned.1.call-start
  14.9 2.0 copy.37
  16.8 4.2 fusion.8.sel_ref
  21.0 0.6 fusion.16.tile_ref
  21.6 55.9 %lookup.1 = bf16[4096,2048]{1,0:T(8,128)(2,1)} custom-call(s32[4096]{0:T(1024)} %fusion.16.tile_ref, s32[4096,1]{1,0:T(8,128)} %fusion.8.sel_ref, bf16[31360,2048]{1,0:T(8,128)(2,1)} %table_ref.1), custom_call_target="tpu_custom_call" | custom-call | flops 335544320000 | bytes 150994944 | tf_op jit(solution)/shard_map/lookup/pallas_call | solution.py:69
  77.6 0.0 all-gather.7.cloned.1.call-done
  77.6 0.0 all-gather.11.cloned.1.call-update
  77.6 0.0 copy-start.4
  77.6 0.0 copy-start.5
  77.8 0.0 copy-start.14
  77.8 0.0 all-gather.13.cloned.1.call-start
  77.8 0.7 all-gather.13.cloned.1.call-update
  78.5 0.0 all-gather.9.cloned.1.call-start
  78.6 2.3 constant_dynamic-slice_fusion.1
  81.0 0.6 broadcast_in_dim.13.pad_ref
  81.7 0.6 dynamic-slice_bitcast_fusion.slope_ref
  82.3 0.6 maximum_convert_fusion.ln_ref
  83.0 0.6 maximum_convert_fusion.1.vec_ref
  83.6 237.5 %chain.1 = (bf16[2,2048,2048]{2,1,0:T(8,128)(2,1)}, bf16[2,256,2048]{2,1,0:T(8,128)(2,1)}) custom-call(bf16[2,2048,2048]{2,1,0:T(8,128)(2,1)} %bitcast.47, f32[4,2048]{1,0:T(4,128)} %maximum_convert_fusion.ln_ref), custom_call_target="tpu_custom_call" | custom-call | flops 1000000 | bytes 67108864 | tf_op jit(solution)/shard_map/chain/pallas_call | solution.py:289
  321.2 0.0 all-gather.11.cloned.1.call-done
  321.2 0.0 all-gather.13.cloned.1.call-done
  321.2 0.0 all-gather.9.cloned.1.call-update
  321.3 18.7 %fusion.2.qkv_ref = bf16[3,2,2,2048,128]{4,3,2,1,0:T(8,128)(2,1)} fusion(f32[3,2,128]{2,1,0:T(2,128)S(1)} %convert_bitcast_fusion, bf16[2,2048,2048]{2,1,0:T(8,128)(2,1)} %get-tuple-element.22, bf16[2048,2,3,128,1]{3,1,2,0,4:T(2,128)(2,1)S(1)} %bitcast.46), kind=kOutput, calls=%fused_computation.3 | convolution fusion | flops 12891193344 | bytes 26217472 | tf_op jit(solution)/shard_map/bsd,dhce->cbhse/dot_general | solution.py:633
  339.9 45.8 %attend.1 = (bf16[2,256,2048]{2,1,0:T(8,128)(2,1)}, bf16[8,8,128]{2,1,0:T(8,128)(2,1)}) custom-call(bf16[3,2,2,2048,128]{4,3,2,1,0:T(8,128)(2,1)} %fusion.2.qkv_ref, s32[2,1,2048]{2,1,0:T(1,128)} %broadcast_in_dim.13.pad_ref, f32[1,2]{1,0:T(1,128)} %dynamic-slice_bitcast_fusion.slope_ref, bf16[8,128]{1,0:T(8,128)(2,1)} %bitcast.51), custom_call_target="tpu_custom_call" | custom-call | flops 30000001024 | bytes 6291456 | tf_op jit(solution)/shard_map/attend/pallas_call | solution.py:397
  385.7 0.7 constant_dynamic-slice_fusion
  386.4 0.6 maximum_convert_fusion.2.bias_ref
  387.0 113.2 %mlp.1 = bf16[512,2048]{1,0:T(8,128)(2,1)} custom-call(bf16[512,2048]{1,0:T(8,128)(2,1)} %bitcast.55, bf16[512,2048]{1,0:T(8,128)(2,1)} %bitcast.54, bf16[4,2048,512]{2,1,0:T(8,128)(2,1)} %bitcast.52, bf16[2048,1024]{1,0:T(8,128)(2,1)} %wup_ref.1, bf16[1024,2048]{1,0:T(8,128)(2,1)} %wdn_ref.1, bf16[4,2048,256]{2,1,0:T(8,128)(2,1)} %bitcast.53, ...), custom_call_target="tpu_custom_call" | custom-call | flops 999999995904 | bytes 40000000 | tf_op jit(solution)/shard_map/mlp/pallas_call | solution.py:585
  500.2 3.3 copy.41
  (46 shorter events, 0.2 us)
Async XLA Ops:
  6.5 314.7 %copy-start = (bf16[2048,2,3,128]{3,1,2,0:T(2,128)(2,1)S(1)}, bf16[2048,2,3,128]{3,1,2,0:T(2,128)(2,1)}, u32[]{:S(2)}) copy-start(bf16[2048,2,3,128]{3,1,2,0:T(2,128)(2,1)} %param.25) | copy-start | bytes 9437188
  6.5 8.3 %copy-start.2 = (s32[2,2048]{1,0:T(2,128)S(1)}, s32[2,2048]{1,0:T(2,128)}, u32[]{:S(2)}) copy-start(s32[2,2048]{1,0:T(2,128)} %param.18) | copy-start | bytes 49156
  6.5 71.1 %all-gather.7.cloned.1.call-start = ((), (), s32[]{:S(2)}) async-start(), calls=%async_computation | async-start | bytes 2359296 | tf_op jit(solution)/shard_map/all_gather | solution.py:620
  9.0 68.6 %collective-permute-start = (bf16[2048,256]{1,0:T(8,128)(2,1)}, bf16[2048,256]{1,0:T(8,128)(2,1)}, u32[]{:S(2)}, u32[]{:S(2)}) collective-permute-start(bf16[2048,256]{1,0:T(8,128)(2,1)} %constant_dynamic-slice_fusion.3), channel_id=1, source_target_pairs={{0,4},{1,5},{2,6},{3,7},{4,0},{5,1},{6,2},{7,3},{8,12},{9,13},{10,... | collective-permute-start | bytes 3145736 | tf_op jit(solution)/shard_map/ppermute | solution.py:621
  14.7 306.4 %all-gather.11.cloned.1.call-start = ((), (), s32[]{:S(2)}) async-start(), calls=%async_computation.2 | async-start | bytes 5242880 | tf_op jit(solution)/shard_map/all_gather | solution.py:628
  77.6 3.2 copy-start.4
  77.6 3.2 copy-start.5
  77.7 3.3 copy-start.6
  77.7 3.3 copy-start.7
  77.7 3.3 copy-start.3
  77.7 3.9 copy-start.12
  77.7 3.9 copy-start.8
  77.7 3.9 copy-start.9
  77.7 3.9 copy-start.10
  77.7 3.9 copy-start.11
  77.8 3.9 copy-start.14
  77.8 4.6 copy-start.13
  77.8 243.4 %all-gather.13.cloned.1.call-start = ((), (), s32[]{:S(2)}) async-start(), calls=%async_computation.3 | async-start | bytes 10485760 | tf_op jit(solution)/shard_map/all_gather | solution.py:627
  78.5 308.5 %all-gather.9.cloned.1.call-start = ((), (), s32[]{:S(2)}) async-start(), calls=%async_computation.1 | async-start | bytes 5242880 | tf_op jit(solution)/shard_map/all_gather | solution.py:632
  80.9 240.3 %collective-permute-start.1 = (bf16[256,2048]{1,0:T(8,128)(2,1)}, bf16[256,2048]{1,0:T(8,128)(2,1)}, u32[]{:S(2)}, u32[]{:S(2)}) collective-permute-start(bf16[256,2048]{1,0:T(8,128)(2,1)} %constant_dynamic-slice_fusion.1), channel_id=1, source_target_pairs={{0,4},{1,5},{2,6},{3,7},{4,0},{5,1},{6,2},{7,3},{8,12},{9,13},{10,... | collective-permute-start | bytes 3145736 | tf_op jit(solution)/shard_map/ppermute | solution.py:622
  500.2 3.3 copy-start.1
Sparse Core Ops, SparseCore 0:
  14.9 49.4 all-gather.6
  77.8 52.0 all-gather.10
  131.7 87.6 all-gather.12
  321.4 51.5 all-gather.8

commit v2 on v1

--- a/solution.py
+++ b/solution.py
@@ -95,9 +95,9 @@
     return (centered * lax.rsqrt(var_v + LN_EPS) * gain + shift).astype(jnp.bfloat16)
 
 
-def chain_kernel(n_tp, part_ref, ln_ref, a_ref, r0_ref, own, pre, rgt, lft, abuf, r0buf,
+def chain_kernel(n_tp, part_a, part_b, ln_ref, a_ref, r0_ref, own, pre, rgt, lft, abuf, r0buf,
                  own_sem, pre_send, pre_recv, r_send, r_recv, l_send, l_recv, a_loc, a_send, a_recv, r0_loc, r0_send, r0_recv):
-    seq = part_ref.shape[1]
+    seq = part_a.shape[0]
     n_chunk = seq // CHUNK
     n_z = n_tp // 2
     me = lax.axis_index("tp")
@@ -130,11 +130,11 @@
     def rows(k):
         return pl.ds(pl.multiple_of(k * CHUNK, CHUNK), CHUNK)
 
-    def own_copy(k):
-        return pltpu.make_async_copy(part_ref.at[c, rows(k), :], own.at[rows(k), :], own_sem.at[k])
-
-    def pre_copy(k):
-        return pltpu.make_async_remote_copy(part_ref.at[1 - c, rows(k), :], pre.at[rows(k), :], pre_send.at[k], pre_recv.at[k], device_id={"tp": peer}, device_id_type=MESH)
+    def own_copy(k, part=part_a):
+        return pltpu.make_async_copy(part.at[rows(k), :], own.at[rows(k), :], own_sem.at[k])
+
+    def pre_copy(k, part=part_a):
+        return pltpu.make_async_remote_copy(part.at[rows(k), :], pre.at[rows(k), :], pre_send.at[k], pre_recv.at[k], device_id={"tp": peer}, device_id_type=MESH)
 
     def right_copy(src, k):
         return pltpu.make_async_remote_copy(src.at[rows(k), :], rgt.at[rows(k), :], r_send.at[k], r_recv.at[k], device_id={"tp": me + 2}, device_id_type=MESH)
@@ -155,8 +155,16 @@
         return pltpu.make_async_remote_copy(r0buf.at[1 - c, rows(i), :], r0_ref.at[c, rows(i), :], r0_send.at[i], r0_recv.at[i], device_id={"tp": peer}, device_id_type=MESH)
 
     def start(k, carry):
-        own_copy(k).start()
-        pre_copy(k).start()
+        @pl.when(c == 0)
+        def _():
+            own_copy(k, part_a).start()
+            pre_copy(k, part_b).start()
+
+        @pl.when(c == 1)
+        def _():
+            own_copy(k, part_b).start()
+            pre_copy(k, part_a).start()
+
         return carry
 
     lax.fori_loop(0, n_chunk, start, 0)
@@ -280,8 +288,9 @@
     lax.fori_loop(0, per_dev, drain_r0, 0)
 
 
-def chain(part, ln_pack, n_tp):
-    n_seq, seq, d = part.shape
+def chain(part_a, part_b, ln_pack, n_tp):
+    n_seq = 2
+    seq, d = part_a.shape
     n_chunk = seq // CHUNK
     per_dev = seq // n_tp // CHUNK
     dma = pltpu.SemaphoreType.DMA
@@ -289,14 +298,14 @@
     return pl.pallas_call(
         functools.partial(chain_kernel, n_tp),
         out_shape=(jax.ShapeDtypeStruct((n_seq, seq, d), jnp.bfloat16), jax.ShapeDtypeStruct((n_seq, seq // n_tp, d), jnp.bfloat16)),
-        in_specs=[pl.BlockSpec(memory_space=pl.ANY), pl.BlockSpec(memory_space=pltpu.VMEM)],
+        in_specs=[pl.BlockSpec(memory_space=pl.ANY), pl.BlockSpec(memory_space=pl.ANY), pl.BlockSpec(memory_space=pltpu.VMEM)],
         out_specs=(pl.BlockSpec(memory_space=pl.ANY), pl.BlockSpec(memory_space=pl.ANY)),
         scratch_shapes=[big, big, big, big, big, pltpu.VMEM((2, seq // n_tp, d), jnp.bfloat16)]
         + [dma((n_chunk,))] * 10 + [dma((per_dev,))] * 3,
         compiler_params=pltpu.CompilerParams(collective_id=0, has_side_effects=True, vmem_limit_bytes=58 * 1024 * 1024),
-        cost_estimate=pl.CostEstimate(flops=10 ** 6, bytes_accessed=8 * part.size, transcendentals=0),
+        cost_estimate=pl.CostEstimate(flops=10 ** 6, bytes_accessed=16 * part_a.size, transcendentals=0),
         name="chain",
-    )(part, ln_pack)
+    )(part_a, part_b, ln_pack)
 
 
 def attend_kernel(n_tp, head_dim, qkv_ref, pad_ref, slope_ref, bup_ref, ctx_ref, ball_ref, cbuf, send_sem, recv_sem, loc_sem, b_send, b_recv, b_loc):
@@ -619,15 +628,16 @@
         swap = [(t, (t + half) % n_tp) for t in range(n_tp)]
         out_part = lax.all_gather(part(w_out, 1), 'tp', axis=0, tiled=True)
         up_part = lax.ppermute(part(w_up, 1), 'tp', swap)
-        down_part = lax.ppermute(part(w_down, 0), 'tp', swap)
-
-        part_emb = lookup(tok_ids.reshape(-1), emb_shard, tp_rank)
-        part_emb = part_emb.reshape(n_seq, seq, d)
-        part_emb, up_part, out_part = lax.optimization_barrier((part_emb, up_part, out_part))
+
+        part_a = lookup(tok_ids[0], emb_shard, tp_rank)
+        ids_b, down_slice, part_a = lax.optimization_barrier((tok_ids[1], part(w_down, 0), part_a))
+        down_part = lax.ppermute(down_slice, 'tp', swap)
+        part_b = lookup(ids_b, emb_shard, tp_rank)
+        part_a, part_b, up_part, out_part = lax.optimization_barrier((part_a, part_b, up_part, out_part))
         wo = lax.all_gather(out_part, 'dp', axis=0, tiled=False)
         wu = lax.all_gather(up_part, 'dp', axis=0, tiled=False)
         ln_pack = jnp.stack([ln_emb_w, ln_emb_b, ln1_w, ln1_b]).astype(f32)
-        normed_all, resid_in = chain(part_emb, ln_pack, n_tp)
+        normed_all, resid_in = chain(part_a, part_b, ln_pack, n_tp)
         normed_all, wu, wo, down_part = lax.optimization_barrier((normed_all, wu, wo, down_part))
         wd = lax.all_gather(down_part, 'dp', axis=0, tiled=True)
         qkv = (jnp.einsum('bsd,dhce->cbhse', normed_all, w_qkv, preferred_element_type=f32) + b_qkv.astype(f32).transpose(1, 0, 2)[:, None, :, None, :]).astype(jnp.bfloat16)

time: 514 us -> 518 us (level)
    pallas_call x1 -> x2, Pallas kernels: 55.9 us -> 59.9 us  [lookup(): pl.pallas_call(lookup_kernel, out_shape=jax.ShapeDtypeStruct((n_tok, d),...]
  transfers between devices with their start and end apart: 6 -> 6, of which waited for: 0 -> 0; matrix products, arithmetic and copies ran while one was open for 7% -> 7% of each run, Pallas kernels for 66% -> 67%
where the time goes in v2:
time: 518 us; the launch traced here: 513 us
  Pallas kernels  455 us (88%)
  matrix products  18.7 us (4%)
  local copies, waits for them, and re-layouts  14.3 us (3%)
  between operations  13.5 us (3%)
  other arithmetic  6.61 us (1%)
    pallas_call x1, Pallas kernels, chain(): pl.pallas_call(functools.partial(chain_kernel, n_tp), out_shape=(jax.Shap...  237 us
    pallas_call x1, Pallas kernels, mlp(): pl.pallas_call(functools.partial(mlp_kernel, n_dp), out_shape=jax.ShapeDt...  112 us
    pallas_call x2, Pallas kernels, lookup(): pl.pallas_call(lookup_kernel, out_shape=jax.ShapeDtypeStruct((n_tok, d),...  59.9 us
    pallas_call x1, Pallas kernels, attend(): pl.pallas_call(functools.partial(attend_kernel, n_tp, head_dim), out_shap...  46.2 us
    dot_general x1, matrix products, local_step(): jnp.einsum('bsd,dhce->cbhse', normed_all, w_qkv, preferred_element_type=f32)  18.7 us
  transfers between devices with their start and end apart: 6, of which 0 were waited for; matrix products, arithmetic and copies ran while one was open for 7% of the time, Pallas kernels for 67%

profile of v2, /device:TPU:0, one launch (start us, length us, event | category | flops | bytes accessed | tf_op | source)
XLA Modules:
  0.0 513.1 jit_solution(17236573009759623464)
XLA Ops:
  6.5 2.4 constant_dynamic-slice_fusion.2
  9.0 4.1 collective-permute-start
  13.0 1.7 constant_dynamic-slice_fusion.1
  14.7 0.0 all-gather.11.cloned.1.call-start
  14.8 2.3 constant_dynamic-slice_fusion.3
  17.1 0.6 slice_subtract_fusion
  17.7 1.3 copy.21
  19.1 2.8 fusion.8.sel_ref
  21.9 0.6 fusion.14.tile_ref
  22.5 30.0 %lookup.2.part_a = bf16[2048,2048]{1,0:T(8,128)(2,1)} custom-call(s32[2048]{0:T(1024)} %fusion.14.tile_ref, s32[2048,1]{1,0:T(8,128)} %fusion.8.sel_ref, bf16[31360,2048]{1,0:T(8,128)(2,1)} %table_ref.3), custom_call_target="tpu_custom_call" | custom-call | flops 167772160000 | bytes 75497472 | tf_op jit(solution)/shard_map/lookup/pallas_call | solution.py:69
  52.5 0.6 fusion.18
  53.1 1.3 copy.26.sel_ref
  54.6 29.9 %lookup.3.part_b = bf16[2048,2048]{1,0:T(8,128)(2,1)} custom-call(s32[2048]{0:T(1024)} %get-tuple-element.42.tile_ref, s32[2048,1]{1,0:T(8,128)} %copy.26.sel_ref, bf16[31360,2048]{1,0:T(8,128)(2,1)} %table_ref.3), custom_call_target="tpu_custom_call" | custom-call | flops 167772160000 | bytes 75497472 | tf_op jit(solution)/shard_map/lookup/pallas_call | solution.py:69
  84.5 0.0 all-gather.7.cloned.1.call-done
  84.5 0.0 all-gather.11.cloned.1.call-update
  84.6 0.0 all-gather.13.cloned.1.call-start
  84.6 0.7 all-gather.13.cloned.1.call-update
  85.3 0.0 all-gather.9.cloned.1.call-start
  85.3 0.1 collective-permute-start.1
  85.5 0.6 broadcast_in_dim.18.pad_ref
  86.3 0.6 dynamic-slice_bitcast_fusion.slope_ref
  86.9 0.7 maximum_convert_fusion.ln_ref
  87.5 0.6 maximum_convert_fusion.1.vec_ref
  88.2 236.7 %chain.1 = (bf16[2,2048,2048]{2,1,0:T(8,128)(2,1)}, bf16[2,256,2048]{2,1,0:T(8,128)(2,1)}) custom-call(bf16[2048,2048]{1,0:T(8,128)(2,1)} %lookup.2.part_a, bf16[2048,2048]{1,0:T(8,128)(2,1)} %lookup.3.part_b, f32[4,2048]{1,0:T(4,128)} %maximum_convert_fusion.ln_ref), custom_call_target="tpu_custom_call" | custom-call | flops 1000000 | bytes 67108864 | tf_op jit(solution)/shard_map/chain/pallas_call | solution.py:298
  324.9 0.0 all-gather.11.cloned.1.call-done
  324.9 0.0 all-gather.13.cloned.1.call-done
  325.0 18.7 %fusion.2.qkv_ref = bf16[3,2,2,2048,128]{4,3,2,1,0:T(8,128)(2,1)} fusion(f32[3,2,128]{2,1,0:T(2,128)S(1)} %convert_bitcast_fusion, bf16[2,2048,2048]{2,1,0:T(8,128)(2,1)} %get-tuple-element.30, bf16[2048,2,3,128,1]{3,1,2,0,4:T(2,128)(2,1)S(1)} %bitcast.26), kind=kOutput, calls=%fused_computation.3 | convolution fusion | flops 12891193344 | bytes 26217472 | tf_op jit(solution)/shard_map/bsd,dhce->cbhse/dot_general | solution.py:643
  343.6 46.2 %attend.1 = (bf16[2,256,2048]{2,1,0:T(8,128)(2,1)}, bf16[8,8,128]{2,1,0:T(8,128)(2,1)}) custom-call(bf16[3,2,2,2048,128]{4,3,2,1,0:T(8,128)(2,1)} %fusion.2.qkv_ref, s32[2,1,2048]{2,1,0:T(1,128)} %broadcast_in_dim.18.pad_ref, f32[1,2]{1,0:T(1,128)} %dynamic-slice_bitcast_fusion.slope_ref, bf16[8,128]{1,0:T(8,128)(2,1)} %bitcast.32), custom_call_target="tpu_custom_call" | custom-call | flops 30000001024 | bytes 6291456 | tf_op jit(solution)/shard_map/attend/pallas_call | solution.py:406
  389.8 0.6 constant_dynamic-slice_fusion
  390.4 0.6 maximum_convert_fusion.2.bias_ref
  391.0 112.4 %mlp.1 = bf16[512,2048]{1,0:T(8,128)(2,1)} custom-call(bf16[512,2048]{1,0:T(8,128)(2,1)} %bitcast.36, bf16[512,2048]{1,0:T(8,128)(2,1)} %bitcast.35, bf16[4,2048,512]{2,1,0:T(8,128)(2,1)} %bitcast.33, bf16[2048,1024]{1,0:T(8,128)(2,1)} %wup_ref.1, bf16[1024,2048]{1,0:T(8,128)(2,1)} %wdn_ref.1, bf16[4,2048,256]{2,1,0:T(8,128)(2,1)} %bitcast.34, ...), custom_call_target="tpu_custom_call" | custom-call | flops 999999995904 | bytes 40000000 | tf_op jit(solution)/shard_map/mlp/pallas_call | solution.py:594
  503.4 3.2 copy.39
  (49 shorter events, 0.2 us)
Async XLA Ops:
  6.5 318.4 %copy-start = (bf16[2048,2,3,128]{3,1,2,0:T(2,128)(2,1)S(1)}, bf16[2048,2,3,128]{3,1,2,0:T(2,128)(2,1)}, u32[]{:S(2)}) copy-start(bf16[2048,2,3,128]{3,1,2,0:T(2,128)(2,1)} %param.25) | copy-start | bytes 9437188
  6.5 10.6 %copy-start.3 = (s32[2,2048]{1,0:T(2,128)S(1)}, s32[2,2048]{1,0:T(2,128)}, u32[]{:S(2)}) copy-start(s32[2,2048]{1,0:T(2,128)} %param.18) | copy-start | bytes 49156
  6.5 78.0 %all-gather.7.cloned.1.call-start = ((), (), s32[]{:S(2)}) async-start(), calls=%async_computation | async-start | bytes 2359296 | tf_op jit(solution)/shard_map/all_gather | solution.py:629
  9.0 75.5 %collective-permute-start = (bf16[2048,256]{1,0:T(8,128)(2,1)}, bf16[2048,256]{1,0:T(8,128)(2,1)}, u32[]{:S(2)}, u32[]{:S(2)}) collective-permute-start(bf16[2048,256]{1,0:T(8,128)(2,1)} %constant_dynamic-slice_fusion.2), channel_id=1, source_target_pairs={{0,4},{1,5},{2,6},{3,7},{4,0},{5,1},{6,2},{7,3},{8,12},{9,13},{10,... | collective-permute-start | bytes 3145736 | tf_op jit(solution)/shard_map/ppermute | solution.py:630
  14.7 310.1 %all-gather.11.cloned.1.call-start = ((), (), s32[]{:S(2)}) async-start(), calls=%async_computation.2 | async-start | bytes 5242880 | tf_op jit(solution)/shard_map/all_gather | solution.py:638
  22.5 30.0 %copy-start.2 = (s32[1,2048]{1,0:T(1,128)S(1)}, s32[1,2048]{1,0:T(1,128)}, u32[]{:S(2)}) copy-start(s32[1,2048]{1,0:T(1,128)} %get-tuple-element.40) | copy-start | bytes 24580
  54.5 31.0 %copy-start.5 = (bf16[2048]{0:T(1024)(128)(2,1)S(1)}, bf16[2048]{0:T(1024)(128)(2,1)}, u32[]{:S(2)}) copy-start(bf16[2048]{0:T(1024)(128)(2,1)} %param.21) | copy-start | bytes 12292
  54.5 31.0 %copy-start.6 = (bf16[2048]{0:T(1024)(128)(2,1)S(1)}, bf16[2048]{0:T(1024)(128)(2,1)}, u32[]{:S(2)}) copy-start(bf16[2048]{0:T(1024)(128)(2,1)} %param.22) | copy-start | bytes 12292
  54.5 31.0 %copy-start.7 = (bf16[2048]{0:T(1024)(128)(2,1)S(1)}, bf16[2048]{0:T(1024)(128)(2,1)}, u32[]{:S(2)}) copy-start(bf16[2048]{0:T(1024)(128)(2,1)} %param.23) | copy-start | bytes 12292
  54.5 31.0 %copy-start.8 = (bf16[2048]{0:T(1024)(128)(2,1)S(1)}, bf16[2048]{0:T(1024)(128)(2,1)}, u32[]{:S(2)}) copy-start(bf16[2048]{0:T(1024)(128)(2,1)} %param.24) | copy-start | bytes 12292
  54.5 31.0 %copy-start.4 = (s32[2,2048]{1,0:T(2,128)S(1)}, s32[2,2048]{1,0:T(2,128)}, u32[]{:S(2)}) copy-start(s32[2,2048]{1,0:T(2,128)} %param.19) | copy-start | bytes 49156
  54.5 31.7 %copy-start.13 = (bf16[1024]{0:T(1024)(128)(2,1)S(1)}, bf16[1024]{0:T(1024)(128)(2,1)}, u32[]{:S(2)}) copy-start(bf16[1024]{0:T(1024)(128)(2,1)} %param.32) | copy-start | bytes 6148
  54.5 31.7 %copy-start.9 = (bf16[2048]{0:T(1024)(128)(2,1)S(1)}, bf16[2048]{0:T(1024)(128)(2,1)}, u32[]{:S(2)}) copy-start(bf16[2048]{0:T(1024)(128)(2,1)} %param.28) | copy-start | bytes 12292
  54.5 31.7 %copy-start.10 = (bf16[2048]{0:T(1024)(128)(2,1)S(1)}, bf16[2048]{0:T(1024)(128)(2,1)}, u32[]{:S(2)}) copy-start(bf16[2048]{0:T(1024)(128)(2,1)} %param.29) | copy-start | bytes 12292
  54.5 31.7 %copy-start.11 = (bf16[2048]{0:T(1024)(128)(2,1)S(1)}, bf16[2048]{0:T(1024)(128)(2,1)}, u32[]{:S(2)}) copy-start(bf16[2048]{0:T(1024)(128)(2,1)} %param.30) | copy-start | bytes 12292
  54.6 31.7 %copy-start.12 = (bf16[2048]{0:T(1024)(128)(2,1)S(1)}, bf16[2048]{0:T(1024)(128)(2,1)}, u32[]{:S(2)}) copy-start(bf16[2048]{0:T(1024)(128)(2,1)} %param.34) | copy-start | bytes 12292
  54.6 31.7 %copy-start.15 = (f32[16]{0:T(128)S(1)}, f32[16]{0:T(128)}, u32[]{:S(2)}) copy-start(f32[16]{0:T(128)} %constant.112.clone) | copy-start | bytes 196
  54.6 32.3 %copy-start.14 = (bf16[2,3,128]{2,0,1:T(2,128)(2,1)S(1)}, bf16[2,3,128]{2,0,1:T(2,128)(2,1)}, u32[]{:S(2)}) copy-start(bf16[2,3,128]{2,0,1:T(2,128)(2,1)} %param.26) | copy-start | bytes 4612
  84.6 240.4 %all-gather.13.cloned.1.call-start = ((), (), s32[]{:S(2)}) async-start(), calls=%async_computation.3 | async-start | bytes 10485760 | tf_op jit(solution)/shard_map/all_gather | solution.py:637
  85.3 305.7 %all-gather.9.cloned.1.call-start = ((), (), s32[]{:S(2)}) async-start(), calls=%async_computation.1 | async-start | bytes 5242880 | tf_op jit(solution)/shard_map/all_gather | solution.py:642
  85.3 239.5 %collective-permute-start.1 = (bf16[256,2048]{1,0:T(8,128)(2,1)}, bf16[256,2048]{1,0:T(8,128)(2,1)}, u32[]{:S(2)}, u32[]{:S(2)}) collective-permute-start(bf16[256,2048]{1,0:T(8,128)(2,1)} %constant_dynamic-slice_fusion.3), channel_id=1, source_target_pairs={{0,4},{1,5},{2,6},{3,7},{4,0},{5,1},{6,2},{7,3},{8,12},{9,13},{10,... | collective-permute-start | bytes 3145736 | tf_op jit(solution)/shard_map/ppermute | solution.py:634
  391.0 115.5 %copy-start.1 = (bf16[2048,2,3,128]{3,1,2,0:T(2,128)(2,1)S(1)}, bf16[2048,2,3,128]{3,1,2,0:T(2,128)(2,1)}, u32[]{:S(2)}) copy-start(bf16[2048,2,3,128]{3,1,2,0:T(2,128)(2,1)} %param.25) | copy-start | bytes 9437188
Sparse Core Ops, SparseCore 0:
  14.9 49.4 all-gather.6
  84.7 51.2 all-gather.10
  137.8 87.6 all-gather.12
  325.1 51.9 all-gather.8
